TPU v7x, 256 devices: a whole 4x4x8 slice. The times are simulated.
256 devices in a mesh: gx: 16 (over x_hi, y, core), vert: 16 (over z, x_lo).
Axes of the slice: x: 4 (x_hi: 2, x_lo: 2; x = x_hi * 2 + x_lo), y: 4, z: 8, core: 2. Of those that a mesh axis runs over, the one named last changes fastest.
Arguments:
- dist: float32 [13824, 64, 256], P('vert', 'gx'), as said below
- offset: int32 [13824], P('vert'), may hold values from -6 to 6, as said below
- fraction: float32 [13824], P('vert'), may hold values from 0 to 1
- cross_velocity: float32 [2, 13824], P(None, 'vert'), may hold values from -4 to 4
- relax: float32 [64, 256], P('gx'), may hold values from 0.3 to 0.9
Outputs:
- updated: float32 [13824, 64, 256], P('vert', 'gx')
Inputs may be any that keep to these rules, and one draw needn't show every extreme that they name: `offset`: each value from -6 to 6 inclusive; both ends are taken by some velocity. `dist`: Positive.
All inputs are finite; a program needn't handle non-finite values.
Results may differ from a plain program's by a relative error of at most 0.0003.
Values sent between devices are 32-bit elements; how exact they have to be, the bound alone decides.
No kernel may reach another device: no remote copies, remote signals or barrier semaphores. Data moves between devices by JAX's collectives and lax.ppermute only.
A program may use at most 64 MiB of HBM per device.

v0:
```python
import jax
import jax.numpy as jnp
from jax import lax
from jax.sharding import Mesh
from jax.sharding import PartitionSpec as P

MAXS = 6
GX = ("gx_0", "gx_1", "gx_2")


def cut_along(array, dim, size):
    before, after = (array.shape[:dim], array.shape[dim + 1 :])
    return jnp.moveaxis(array.reshape(*before, size, -1, *after), dim, 0)


def laid_out(parts, dim):
    parts = jnp.moveaxis(parts, 0, dim)
    lengths = parts.shape
    return parts.reshape(*lengths[:dim], lengths[dim] * lengths[dim + 1], *lengths[dim + 2 :])


def turned_blocks(parts, axes, sequence):
    lengths = [lax.axis_size(a) for a in axes]
    parts = parts.reshape(*lengths, *parts.shape[1:])
    for k in sequence:
        parts = lax.all_to_all(parts, axes[k], split_axis=k, concat_axis=k, tiled=True)
    return parts.reshape(-1, *parts.shape[len(axes) :])


def exchange_by_chip(array, groups, sequence, split_dim, concat_dim):
    size = lax.axis_size(groups[0]) * lax.axis_size(groups[1])
    parts = cut_along(array, split_dim, size)
    return laid_out(turned_blocks(parts, groups, sequence), concat_dim)


def sent_to_all(array, axis):
    copies = jnp.broadcast_to(array, (lax.axis_size(axis), *array.shape))
    return lax.all_to_all(copies, axis, split_axis=0, concat_axis=0, tiled=True)


def of_everyone(array, axis):
    return sent_to_all(array, axis).sum(axis=0)


def stencil_matrix(offset, fraction, row_count, col_count):
    position = 1.0 - fraction
    weights = jnp.stack(
        [
            -position * (position - 1.0) * (position - 2.0) / 6.0,
            (position + 1.0) * (position - 1.0) * (position - 2.0) / 2.0,
            -(position + 1.0) * position * (position - 2.0) / 2.0,
            (position + 1.0) * position * (position - 1.0) / 6.0,
        ],
        axis=1,
    )
    row_index = jnp.arange(row_count, dtype=jnp.int32)
    tap_index = jnp.arange(4, dtype=jnp.int32)
    target = jnp.mod(
        row_index[None, :, None] - offset[:, None, None] - 2 + tap_index[None, None, :], col_count
    )
    onehot = (target[..., None] == jnp.arange(col_count, dtype=jnp.int32)).astype(weights.dtype)
    return jnp.einsum("vrjc,vj->vrc", onehot, weights, precision=lax.Precision.HIGHEST)


def velocities(offset, fraction, cross_velocity):
    along = (offset.astype(fraction.dtype) + fraction) * (3.0 / MAXS)
    return (along, cross_velocity[0], cross_velocity[1])


def cell_state(sums):
    density = sums[0]
    mean_x = sums[1] / density
    mean_y = sums[2] / density
    mean_z = sums[3] / density
    temper = (sums[4] / density - (mean_x * mean_x + mean_y * mean_y + mean_z * mean_z)) / 3.0
    return jnp.stack([density, mean_x, mean_y, mean_z, temper])


def equilibrium(vel_x, vel_y, vel_z, state):
    diff_x = vel_x[:, None, None] - state[1]
    diff_y = vel_y[:, None, None] - state[2]
    diff_z = vel_z[:, None, None] - state[3]
    return jnp.exp(-(diff_x * diff_x + diff_y * diff_y + diff_z * diff_z) / (2.0 * state[4]))


def per_device(dist, offset, fraction, cross_velocity, relax):
    local_vel, local_cells, window = dist.shape
    group_count = lax.axis_size(GX)
    subset = local_vel // group_count
    start = lax.axis_index(GX) * subset
    lines = lax.all_to_all(dist, GX, split_axis=0, concat_axis=1, tiled=True)
    line_cells = local_cells * group_count
    shift_part = lax.dynamic_slice_in_dim(offset, start, subset)
    frac_part = lax.dynamic_slice_in_dim(fraction, start, subset)
    matrix = stencil_matrix(shift_part, frac_part, line_cells, line_cells)
    moved = jnp.einsum("vrc,vcn->vrn", matrix, lines, precision=lax.Precision.HIGHEST)
    shifted = exchange_by_chip(moved, (("gx_0", "gx_1"), "gx_2"), (1, 0), 1, 0)
    vel_x, vel_y, vel_z = velocities(offset, fraction, cross_velocity)
    coeffs = jnp.stack(
        [jnp.ones_like(vel_x), vel_x, vel_y, vel_z, vel_x * vel_x + vel_y * vel_y + vel_z * vel_z]
    )
    partial_sums = jnp.einsum("mv,vxn->mxn", coeffs, shifted, precision=lax.Precision.HIGHEST)
    state = cell_state(of_everyone(partial_sums, "vert"))
    weight = equilibrium(vel_x, vel_y, vel_z, state)
    total = of_everyone(jnp.sum(weight, axis=0), "vert")
    return shifted + relax[None] * (state[0] * weight / total - shifted)


def solution(mesh):
    torus = Mesh(
        mesh.devices.reshape(2, 4, 2, mesh.shape["vert"]), ("gx_0", "gx_1", "gx_2", "vert")
    )
    placed = (P("vert", GX, None), P("vert"), P("vert"), P(None, "vert"), P(GX, None))
    return jax.shard_map(
        per_device, mesh=torus, in_specs=placed, out_specs=P("vert", GX, None), check_vma=False
    )
```

profile of v0, /device:TPU:4, one launch (start us, length us, event | category | flops | bytes accessed | tf_op | source)
XLA Modules:
  0.0 182.1 jit_solution(566256399795120523)
XLA Ops:
  0.0 7.5 %all-to-all-start = ((f32[864,4,256]{2,1,0:T(4,128)}), f32[864,4,256]{2,1,0:T(4,128)S(1)}, u32[]{:S(2)}, u32[]{:S(2)}) async-start(f32[864,4,256]{2,1,0:T(4,128)} %param.5), calls=%async_computation | async-start | bytes 7077888 | tf_op jit(solution)/shard_map/all_to_all | solution.py:91
  7.5 0.8 multiply_bitcast_fusion.4
  8.9 0.8 dynamic_slice.6
  10.5 2.7 %copy.34 = s32[54,64,4]{2,1,0:T(8,128)} copy(s32[54,64,4]{1,2,0:T(4,128)} %add_select_fusion) | data formatting | bytes 110592 | tf_op jit(solution)/shard_map/jit(remainder)/select_n | solution.py:58
  13.2 12.8 %fusion = f32[54,1,64,64]{3,1,2,0:T(1,128)} fusion(f32[54,4,1,1]{1,2,3,0:T(1,128)} %copy.44, s32[54,64,4]{2,1,0:T(8,128)} %copy.34), kind=kOutput, calls=%fused_computation.1 | convolution fusion | flops 11501568 | bytes 940896 | tf_op jit(solution)/shard_map/vrjc,vj->vrc/dot_general | solution.py:62
  26.0 24.0 %all-to-all-done = f32[864,4,256]{2,1,0:T(4,128)S(1)} async-done(((f32[864,4,256]{2,1,0:T(4,128)}), f32[864,4,256]{2,1,0:T(4,128)S(1)}, u32[]{:S(2)}, u32[]{:S(2)}) %all-to-all-start) | async-done | bytes 3538976 | tf_op jit(solution)/shard_map/all_to_all | solution.py:91
  50.0 2.8 %copy.59 = f32[16,54,4,256]{3,2,0,1:T(4,128)} copy(f32[16,54,4,256]{3,2,1,0:T(4,128)S(1)} %bitcast.42) | data formatting | bytes 7077888 | tf_op jit(solution)/shard_map/all_to_all | solution.py:91
  52.8 3.4 %all_to_all.28 = f32[54,64,256]{2,1,0:T(8,128)S(1)} reshape(f32[54,16,4,256]{3,2,1,0:T(4,128)} %bitcast.43) | data formatting | bytes 7077888 | tf_op jit(solution)/shard_map/all_to_all | solution.py:91
  56.2 4.9 %fusion.17 = f32[54,64,256]{2,1,0:T(8,128)S(1)} fusion(f32[54,64,64]{2,1,0:T(8,128)} %bitcast.44, f32[54,64,256]{2,1,0:T(8,128)S(1)} %all_to_all.28), kind=kOutput, calls=%fused_computation.45 | convolution fusion | flops 679477248 | bytes 7962624 | tf_op jit(solution)/shard_map/vrc,vcn->vrn/dot_general | solution.py:96
  61.1 2.1 %copy.46 = f32[54,64,256]{2,0,1:T(8,128)S(1)} copy(f32[54,64,256]{2,1,0:T(8,128)S(1)} %fusion.17) | data formatting | bytes 7077888 | tf_op jit(solution)/shard_map/reshape | solution.py:13
  63.1 2.1 %copy.37 = f32[8,2,54,4,256]{4,0,3,2,1:T(8,128)S(1)} copy(f32[8,2,54,4,256]{4,2,3,1,0:T(8,128)S(1)} %bitcast.41) | data formatting | bytes 7077888 | tf_op jit(solution)/shard_map/reshape | solution.py:24
  65.2 6.6 %all_to_all.38 = f32[8,2,54,4,256]{4,0,3,2,1:T(8,128)S(1)} all-to-all(f32[8,2,54,4,256]{4,0,3,2,1:T(8,128)S(1)} %copy.37), channel_id=1, replica_groups=mesh['gx_0'=2,'gx_1'=4,'gx_2'=2,'vert'=16] {'gx_2'}, dimensions={1} | all-to-all | bytes 7077888 | tf_op jit(solution)/shard_map/all_to_all | solution.py:26
  71.8 3.2 %copy.38 = f32[8,2,54,4,256]{4,3,2,1,0:T(4,128)} copy(f32[8,2,54,4,256]{4,0,3,2,1:T(8,128)S(1)} %all_to_all.38) | data formatting | bytes 7077888 | tf_op jit(solution)/shard_map/all_to_all | solution.py:26
  74.9 15.8 %all-to-all-start.2 = ((f32[8,2,54,4,256]{4,3,2,1,0:T(4,128)}), f32[8,2,54,4,256]{4,3,2,1,0:T(4,128)S(1)}, u32[]{:S(2)}, u32[]{:S(2)}) async-start(f32[8,2,54,4,256]{4,3,2,1,0:T(4,128)} %copy.38), calls=%async_computation.2 | async-start | bytes 7077888 | tf_op jit(solution)/shard_map/all_to_all | solution.py:26
  92.6 39.4 %all-to-all-done.2 = f32[8,2,54,4,256]{4,3,2,1,0:T(4,128)S(1)} async-done(((f32[8,2,54,4,256]{4,3,2,1,0:T(4,128)}), f32[8,2,54,4,256]{4,3,2,1,0:T(4,128)S(1)}, u32[]{:S(2)}, u32[]{:S(2)}) %all-to-all-start.2) | async-done | bytes 3538976 | tf_op jit(solution)/shard_map/all_to_all | solution.py:26
  131.9 2.9 %fusion.2 = f32[5,4,256]{2,0,1:T(8,128)S(1)} fusion(f32[864,4,256]{2,1,0:T(4,128)S(1)} %bitcast.39, f32[1,864]{1,0:T(1,128)} %stack.34, f32[2,864]{1,0:T(2,128)} %param.8, f32[1,864]{1,0:T(1,128)S(1)} %stack.33, f32[5]{0:T(128)} %pad.clone), kind=kOutput, calls=%fused_computation.6 | convolution fusion | flops 53097120 | bytes 3573268 | tf_op jit(solution)/shard_map/mv,vxn->mxn/dot_general | solution.py:102
  134.9 21.6 %all_to_all.39 = f32[16,5,4,256]{3,2,1,0:T(4,128)} all-to-all(f32[16,5,4,256]{3,2,1,0:T(4,128)S(1)} %broadcast_in_dim.4), channel_id=1, replica_groups=mesh['gx_0'=2,'gx_1'=4,'gx_2'=2,'vert'=16] {'vert'}, dimensions={0} | all-to-all | bytes 655360 | tf_op jit(solution)/shard_map/all_to_all | solution.py:38
  156.5 1.6 reduce_sum.27
  158.1 0.8 slice_bitcast_fusion
  159.5 1.7 fusion.4
  161.2 12.4 %all_to_all.40 = f32[16,4,256]{2,1,0:T(4,128)} all-to-all(f32[16,4,256]{2,1,0:T(4,128)S(1)} %broadcast_in_dim.5), channel_id=1, replica_groups=mesh['gx_0'=2,'gx_1'=4,'gx_2'=2,'vert'=16] {'vert'}, dimensions={0} | all-to-all | bytes 131072 | tf_op jit(solution)/shard_map/all_to_all | solution.py:38
  173.6 1.5 reduce_sum.29
  175.0 3.0 %multiply_add_fusion = f32[864,4,256]{2,0,1:T(8,128)S(1)} fusion(f32[864,4,256]{2,1,0:T(4,128)S(1)} %bitcast.40, f32[4,256]{1,0:T(4,128)} %reduce_sum.29, f32[4,256]{1,0:T(4,128)} %copy-done.4, f32[4,256]{1,0:T(4,128)} %copy-done.1, f32[864]{0:T(1024)S(1)} %get-tuple-element.6, f32[4,256]{1,0:T(4,128)} %copy-done.2, f32[864]{0:T(1024)S(1)} %get-tuple-element.5, ...), kind=kLoop, calls=%fused_computation.3 | loop fusion | flops 13271040 | bytes 7116928 | tf_op jit(solution)/shard_map/add | solution.py:106
  178.0 4.1 %copy.43 = f32[864,4,256]{2,1,0:T(4,128)} copy(f32[864,4,256]{2,0,1:T(8,128)S(1)} %multiply_add_fusion) | data formatting | bytes 7077888 | tf_op jit(solution)/shard_map/add | solution.py:106
  (23 shorter events, 4.0 us)
Async XLA Ops:
  0.0 50.0 %all-to-all-start = ((f32[864,4,256]{2,1,0:T(4,128)}), f32[864,4,256]{2,1,0:T(4,128)S(1)}, u32[]{:S(2)}, u32[]{:S(2)}) async-start(f32[864,4,256]{2,1,0:T(4,128)} %param.5), calls=%async_computation | async-start | bytes 7077888 | tf_op jit(solution)/shard_map/all_to_all | solution.py:91
  74.9 15.8 %copy-start = (f32[2,864]{1,0:T(2,128)S(1)}, f32[2,864]{1,0:T(2,128)}, u32[]{:S(2)}) copy-start(f32[2,864]{1,0:T(2,128)} %param.8) | copy-start | bytes 20740
  74.9 57.0 %all-to-all-start.2 = ((f32[8,2,54,4,256]{4,3,2,1,0:T(4,128)}), f32[8,2,54,4,256]{4,3,2,1,0:T(4,128)S(1)}, u32[]{:S(2)}, u32[]{:S(2)}) async-start(f32[8,2,54,4,256]{4,3,2,1,0:T(4,128)} %copy.38), calls=%async_computation.2 | async-start | bytes 7077888 | tf_op jit(solution)/shard_map/all_to_all | solution.py:26
  158.9 0.6 copy-start.1
  158.9 2.3 %copy-start.2 = (f32[4,256]{1,0:T(4,128)}, f32[4,256]{1,0:T(4,128)S(1)}, u32[]{:S(2)}) copy-start(f32[4,256]{1,0:T(4,128)S(1)} %get-tuple-element.13) | copy-start | bytes 12292
  158.9 2.3 %copy-start.3 = (f32[4,256]{1,0:T(4,128)}, f32[4,256]{1,0:T(4,128)S(1)}, u32[]{:S(2)}) copy-start(f32[4,256]{1,0:T(4,128)S(1)} %get-tuple-element.14) | copy-start | bytes 12292
  158.9 2.3 %copy-start.4 = (f32[4,256]{1,0:T(4,128)}, f32[4,256]{1,0:T(4,128)S(1)}, u32[]{:S(2)}) copy-start(f32[4,256]{1,0:T(4,128)S(1)} %get-tuple-element.15) | copy-start | bytes 12292
where the time goes:
time: 183 us; the launch traced here: 182 us
  waiting for transfers between devices  63.3 us (35%)
  blocking collectives  40.5 us (22%)
  local copies, waits for them, and re-layouts  23.4 us (13%)
  starting transfers between devices  23.2 us (13%)
  matrix products  20.6 us (11%)
  other arithmetic  10.8 us (6%)
    all_to_all x1, waiting for transfers between devices, turned_blocks(): lax.all_to_all(parts, axes[k], split_axis=k, concat_axis=k, tiled=True)  39.4 us
    all_to_all x2, blocking collectives, sent_to_all(): return lax.all_to_all(copies, axis, split_axis=0, concat_axis=0, tiled=True)  33.9 us
    all_to_all x1, waiting for transfers between devices, per_device(): lines = lax.all_to_all(dist, GX, split_axis=0, concat_axis=1, tiled=True)  24 us
    all_to_all x1, starting transfers between devices, turned_blocks(): lax.all_to_all(parts, axes[k], split_axis=k, concat_axis=k, tiled=True)  15.8 us
    dot_general x1, matrix products, stencil_matrix(): jnp.einsum('vrjc,vj->vrc', onehot, weights, precision=lax.Precision.HIGHEST)  12.8 us
    all_to_all x1, starting transfers between devices, per_device(): lines = lax.all_to_all(dist, GX, split_axis=0, concat_axis=1, tiled=True)  7.45 us
    all_to_all x1, blocking collectives, turned_blocks(): lax.all_to_all(parts, axes[k], split_axis=k, concat_axis=k, tiled=True)  6.58 us
    all_to_all x2, local copies, waits for them, and re-layouts, per_device(): lines = lax.all_to_all(dist, GX, split_axis=0, concat_axis=1, tiled=True)  6.18 us
  transfers between devices with their start and end apart: 2, of which 2 were waited for; matrix products, arithmetic and copies ran while one was open for 11% of the time, Pallas kernels for 0%

commit v1 on v0

--- a/solution.py
+++ b/solution.py
@@ -6,6 +6,18 @@
 
 MAXS = 6
 GX = ("gx_0", "gx_1", "gx_2")
+
+
+def _convert_words(my_tile, row_axis):
+    return jnp.concatenate(
+        lax.all_to_all(
+            jnp.stack(jnp.split(my_tile, lax.axis_size(row_axis), axis=0), 0),
+            split_axis=0,
+            axis_name=row_axis,
+            concat_axis=0,
+        ),
+        axis=1,
+    )
 
 
 def cut_along(array, dim, size):
@@ -88,7 +100,7 @@
     group_count = lax.axis_size(GX)
     subset = local_vel // group_count
     start = lax.axis_index(GX) * subset
-    lines = lax.all_to_all(dist, GX, split_axis=0, concat_axis=1, tiled=True)
+    lines = _convert_words(dist, GX)
     line_cells = local_cells * group_count
     shift_part = lax.dynamic_slice_in_dim(offset, start, subset)
     frac_part = lax.dynamic_slice_in_dim(fraction, start, subset)

time: 183 us -> 209 us (1.14)
  local copies, waits for them, and re-layouts: 23.4 us -> 49.6 us
    unnamed x10 -> x25, local copies, waits for them, and re-layouts: 0.57 us -> 25.1 us
    reshape x0 -> x2, local copies, waits for them, and re-layouts: none -> 6.18 us  [_convert_words(): jnp.concatenate(lax.all_to_all(jnp.stack(jnp.split(my_tile, lax.axis_size...]
    all_to_all x2 -> x0, local copies, waits for them, and re-layouts: 6.18 us -> none  [per_device(): lines = lax.all_to_all(dist, GX, split_axis=0, concat_axis=1, tiled=True)]
  transfers between devices with their start and end apart: 2 -> 2, of which waited for: 2 -> 2; matrix products, arithmetic and copies ran while one was open for 11% -> 10% of each run, Pallas kernels for 0% -> 0%
where the time goes in v1:
time: 209 us; the launch traced here: 208 us
  waiting for transfers between devices  63.4 us (30%)
  local copies, waits for them, and re-layouts  49.6 us (24%)
  blocking collectives  40.5 us (19%)
  starting transfers between devices  23.2 us (11%)
  matrix products  20.6 us (10%)
  other arithmetic  10.8 us (5%)
    all_to_all x1, waiting for transfers between devices, turned_blocks(): lax.all_to_all(parts, axes[k], split_axis=k, concat_axis=k, tiled=True)  39.4 us
    all_to_all x2, blocking collectives, sent_to_all(): return lax.all_to_all(copies, axis, split_axis=0, concat_axis=0, tiled=True)  33.9 us
    unnamed x25, local copies, waits for them, and re-layouts  25.1 us
    all_to_all x1, waiting for transfers between devices, _convert_words(): lax.all_to_all(jnp.stack(jnp.split(my_tile, lax.axis_size(row_axis), axis...  24 us
    all_to_all x1, starting transfers between devices, turned_blocks(): lax.all_to_all(parts, axes[k], split_axis=k, concat_axis=k, tiled=True)  15.8 us
    dot_general x1, matrix products, stencil_matrix(): jnp.einsum('vrjc,vj->vrc', onehot, weights, precision=lax.Precision.HIGHEST)  12.8 us
    all_to_all x1, starting transfers between devices, _convert_words(): lax.all_to_all(jnp.stack(jnp.split(my_tile, lax.axis_size(row_axis), axis...  7.45 us
    all_to_all x1, blocking collectives, turned_blocks(): lax.all_to_all(parts, axes[k], split_axis=k, concat_axis=k, tiled=True)  6.58 us
  transfers between devices with their start and end apart: 2, of which 2 were waited for; matrix products, arithmetic and copies ran while one was open for 10% of the time, Pallas kernels for 0%

profile of v1, /device:TPU:4, one launch (start us, length us, event | category | flops | bytes accessed | tf_op | source)
XLA Modules:
  0.0 208.2 jit_solution(2643114164208156274)
XLA Ops:
  0.0 1.6 bitcast_dynamic-update-slice_fusion.15
  1.6 1.6 bitcast_dynamic-update-slice_fusion.14
  8.2 1.6 bitcast_dynamic-update-slice_fusion.10
  9.8 1.6 bitcast_dynamic-update-slice_fusion.9
  26.2 7.5 %all-to-all-start = ((f32[16,54,4,256]{3,2,1,0:T(4,128)}), f32[16,54,4,256]{3,2,1,0:T(4,128)S(1)}, u32[]{:S(2)}, u32[]{:S(2)}) async-start(f32[16,54,4,256]{3,2,1,0:T(4,128)} %bitcast_dynamic-update-slice_fusion), calls=%async_computation | async-start | bytes 7077888 | tf_op jit(solution)/shard_map/all_to_all | solution.py:13
  36.7 2.7 %copy.34 = s32[54,64,4]{2,1,0:T(8,128)} copy(s32[54,64,4]{1,2,0:T(4,128)} %add_select_fusion) | data formatting | bytes 110592 | tf_op jit(solution)/shard_map/jit(remainder)/select_n | solution.py:70
  39.4 12.8 %fusion = f32[54,1,64,64]{3,1,2,0:T(1,128)} fusion(f32[54,4,1,1]{1,2,3,0:T(1,128)} %copy.44, s32[54,64,4]{2,1,0:T(8,128)} %copy.34), kind=kOutput, calls=%fused_computation.1 | convolution fusion | flops 11501568 | bytes 940896 | tf_op jit(solution)/shard_map/vrjc,vj->vrc/dot_general | solution.py:74
  52.1 24.0 %all-to-all-done = f32[16,54,4,256]{3,2,1,0:T(4,128)S(1)} async-done(((f32[16,54,4,256]{3,2,1,0:T(4,128)}), f32[16,54,4,256]{3,2,1,0:T(4,128)S(1)}, u32[]{:S(2)}, u32[]{:S(2)}) %all-to-all-start) | async-done | bytes 3538976 | tf_op jit(solution)/shard_map/all_to_all | solution.py:13
  76.1 2.8 %copy.35 = f32[54,16,4,256]{3,2,1,0:T(4,128)} copy(f32[54,16,4,256]{3,2,0,1:T(4,128)S(1)} %bitcast.71) | data formatting | bytes 7077888 | tf_op jit(solution)/shard_map/reshape | solution.py:12
  78.9 3.4 %reshape.59 = f32[54,64,256]{2,1,0:T(8,128)S(1)} reshape(f32[54,16,4,256]{3,2,1,0:T(4,128)} %copy.35) | data formatting | bytes 7077888 | tf_op jit(solution)/shard_map/reshape | solution.py:12
  82.3 4.9 %fusion.17 = f32[54,64,256]{2,1,0:T(8,128)S(1)} fusion(f32[54,64,64]{2,1,0:T(8,128)} %bitcast.72, f32[54,64,256]{2,1,0:T(8,128)S(1)} %reshape.59), kind=kOutput, calls=%fused_computation.60 | convolution fusion | flops 679477248 | bytes 7962624 | tf_op jit(solution)/shard_map/vrc,vcn->vrn/dot_general | solution.py:108
  87.2 2.1 copy.46
  89.3 2.1 copy.37
  91.4 6.6 %all_to_all.25 = f32[8,2,54,4,256]{4,0,3,2,1:T(8,128)S(1)} all-to-all(f32[8,2,54,4,256]{4,0,3,2,1:T(8,128)S(1)} %copy.37), channel_id=1, replica_groups=mesh['gx_0'=2,'gx_1'=4,'gx_2'=2,'vert'=16] {'gx_2'}, dimensions={1} | all-to-all | bytes 7077888 | tf_op jit(solution)/shard_map/all_to_all | solution.py:38
  97.9 3.2 %copy.38 = f32[8,2,54,4,256]{4,3,2,1,0:T(4,128)} copy(f32[8,2,54,4,256]{4,0,3,2,1:T(8,128)S(1)} %all_to_all.25) | data formatting | bytes 7077888 | tf_op jit(solution)/shard_map/all_to_all | solution.py:38
  101.1 15.8 %all-to-all-start.2 = ((f32[8,2,54,4,256]{4,3,2,1,0:T(4,128)}), f32[8,2,54,4,256]{4,3,2,1,0:T(4,128)S(1)}, u32[]{:S(2)}, u32[]{:S(2)}) async-start(f32[8,2,54,4,256]{4,3,2,1,0:T(4,128)} %copy.38), calls=%async_computation.2 | async-start | bytes 7077888 | tf_op jit(solution)/shard_map/all_to_all | solution.py:38
  118.7 39.4 %all-to-all-done.2 = f32[8,2,54,4,256]{4,3,2,1,0:T(4,128)S(1)} async-done(((f32[8,2,54,4,256]{4,3,2,1,0:T(4,128)}), f32[8,2,54,4,256]{4,3,2,1,0:T(4,128)S(1)}, u32[]{:S(2)}, u32[]{:S(2)}) %all-to-all-start.2) | async-done | bytes 3538976 | tf_op jit(solution)/shard_map/all_to_all | solution.py:38
  158.1 2.9 %fusion.2 = f32[5,4,256]{2,0,1:T(8,128)S(1)} fusion(f32[864,4,256]{2,1,0:T(4,128)S(1)} %bitcast.68, f32[1,864]{1,0:T(1,128)} %stack.102, f32[2,864]{1,0:T(2,128)} %param.8, f32[1,864]{1,0:T(1,128)S(1)} %stack.101, f32[5]{0:T(128)} %pad.clone), kind=kOutput, calls=%fused_computation.5 | convolution fusion | flops 53097120 | bytes 3573268 | tf_op jit(solution)/shard_map/mv,vxn->mxn/dot_general | solution.py:114
  161.1 21.6 %all_to_all.26 = f32[16,5,4,256]{3,2,1,0:T(4,128)} all-to-all(f32[16,5,4,256]{3,2,1,0:T(4,128)S(1)} %broadcast_in_dim.4), channel_id=1, replica_groups=mesh['gx_0'=2,'gx_1'=4,'gx_2'=2,'vert'=16] {'vert'}, dimensions={0} | all-to-all | bytes 655360 | tf_op jit(solution)/shard_map/all_to_all | solution.py:50
  182.6 1.6 reduce_sum.27
  185.6 1.7 fusion.4
  187.4 12.4 %all_to_all.27 = f32[16,4,256]{2,1,0:T(4,128)} all-to-all(f32[16,4,256]{2,1,0:T(4,128)S(1)} %broadcast_in_dim.5), channel_id=1, replica_groups=mesh['gx_0'=2,'gx_1'=4,'gx_2'=2,'vert'=16] {'vert'}, dimensions={0} | all-to-all | bytes 131072 | tf_op jit(solution)/shard_map/all_to_all | solution.py:50
  201.2 3.0 %multiply_add_fusion = f32[864,4,256]{2,0,1:T(8,128)S(1)} fusion(f32[864,4,256]{2,1,0:T(4,128)S(1)} %bitcast.69, f32[4,256]{1,0:T(4,128)} %reduce_sum.29, f32[4,256]{1,0:T(4,128)} %copy-done.4, f32[4,256]{1,0:T(4,128)} %copy-done.1, f32[864]{0:T(1024)S(1)} %get-tuple-element.6, f32[4,256]{1,0:T(4,128)} %copy-done.2, f32[864]{0:T(1024)S(1)} %get-tuple-element.5, ...), kind=kLoop, calls=%fused_computation.2 | loop fusion | flops 13271040 | bytes 7116928 | tf_op jit(solution)/shard_map/add | solution.py:118
  204.1 4.1 %copy.43 = f32[864,4,256]{2,1,0:T(4,128)} copy(f32[864,4,256]{2,0,1:T(8,128)S(1)} %multiply_add_fusion) | data formatting | bytes 7077888 | tf_op jit(solution)/shard_map/add | solution.py:118
  (39 shorter events, 27.4 us)
Async XLA Ops:
  26.2 50.0 %all-to-all-start = ((f32[16,54,4,256]{3,2,1,0:T(4,128)}), f32[16,54,4,256]{3,2,1,0:T(4,128)S(1)}, u32[]{:S(2)}, u32[]{:S(2)}) async-start(f32[16,54,4,256]{3,2,1,0:T(4,128)} %bitcast_dynamic-update-slice_fusion), calls=%async_computation | async-start | bytes 7077888 | tf_op jit(solution)/shard_map/all_to_all | solution.py:13
  101.1 15.8 %copy-start = (f32[2,864]{1,0:T(2,128)S(1)}, f32[2,864]{1,0:T(2,128)}, u32[]{:S(2)}) copy-start(f32[2,864]{1,0:T(2,128)} %param.8) | copy-start | bytes 20740
  101.1 57.0 %all-to-all-start.2 = ((f32[8,2,54,4,256]{4,3,2,1,0:T(4,128)}), f32[8,2,54,4,256]{4,3,2,1,0:T(4,128)S(1)}, u32[]{:S(2)}, u32[]{:S(2)}) async-start(f32[8,2,54,4,256]{4,3,2,1,0:T(4,128)} %copy.38), calls=%async_computation.2 | async-start | bytes 7077888 | tf_op jit(solution)/shard_map/all_to_all | solution.py:38
  185.0 0.6 copy-start.1
  185.0 2.3 %copy-start.2 = (f32[4,256]{1,0:T(4,128)}, f32[4,256]{1,0:T(4,128)S(1)}, u32[]{:S(2)}) copy-start(f32[4,256]{1,0:T(4,128)S(1)} %get-tuple-element.13) | copy-start | bytes 12292
  185.0 2.3 %copy-start.3 = (f32[4,256]{1,0:T(4,128)}, f32[4,256]{1,0:T(4,128)S(1)}, u32[]{:S(2)}) copy-start(f32[4,256]{1,0:T(4,128)S(1)} %get-tuple-element.14) | copy-start | bytes 12292
  185.0 2.3 %copy-start.4 = (f32[4,256]{1,0:T(4,128)}, f32[4,256]{1,0:T(4,128)S(1)}, u32[]{:S(2)}) copy-start(f32[4,256]{1,0:T(4,128)S(1)} %get-tuple-element.15) | copy-start | bytes 12292
